TPU v7x, 128 devices: a whole 4x4x4 slice. The times are simulated.
128 devices in a mesh: row: 8 (over y, core), col: 16 (over x, z).
Axes of the slice: x: 4, y: 4, z: 4, core: 2. Of those that a mesh axis runs over, the one named last changes fastest.
Arguments:
- matrix_in: float32 [4, 4096, 2, 8192], P(None, 'row', None, 'col'), as said below
- panel_start: int32 [1], replicated, may hold values from 0 to 29
Outputs:
- matrix_out: float32 [4, 4096, 2, 8192], P(None, 'row', None, 'col')
Inputs may be any that keep to these rules, and one draw needn't show every extreme that they name: matrix_in is symmetric and positive definite.
All inputs are finite; a program needn't handle non-finite values.
Results may differ from a plain program's by a relative error of at most 0.0001.
Values sent between devices are 32-bit elements.
No kernel may reach another device: no remote copies, remote signals or barrier semaphores. Data moves between devices by JAX's collectives and lax.ppermute only.
A program may use at most 128 MiB of HBM per device.

v0:
```python
import jax
import jax.numpy as jnp
from jax import lax
from jax.sharding import PartitionSpec as P


def picked(x, axis, root):
    return lax.dynamic_index_in_dim(lax.all_gather(x, axis), root, 0, keepdims=False)


def from_root(value, axis, source):
    kept = jnp.where(lax.axis_index(axis) == source, value, 0).astype(value.dtype)
    return lax.psum(kept, axis)


def padded_to(lines, length):
    spare = -lines.shape[0] % length
    if not spare:
        return lines
    return jnp.concatenate([lines, jnp.zeros((spare, *lines.shape[1:]), lines.dtype)])


def broadcast_by_parts(x, axis, root):
    lines = jnp.where(lax.axis_index(axis) == root, x, jnp.zeros_like(x)).reshape(
        -1, *x.shape[1:][-1:]
    )
    padded = padded_to(lines, lax.axis_size(axis))
    own = lax.psum_scatter(padded, axis, scatter_dimension=0, tiled=True)
    return lax.all_gather(own, axis, axis=0, tiled=True)[: len(lines)].reshape(x.shape)


def update(matrix, rows_part, cols_part):
    loc_rows, width, _unused_a = rows_part.shape
    loc_cols = cols_part.shape[0]
    left_panel = rows_part.reshape(loc_rows * width, width)
    right_panel = cols_part.reshape(loc_cols * width, width)
    product = lax.dot_general(
        left_panel,
        right_panel,
        (((1,), (1,)), ((), ())),
        precision=lax.Precision.HIGHEST,
        preferred_element_type=jnp.float32,
    )
    return matrix - product.reshape(loc_rows, width, loc_cols, width)


def factor_panel(matrix, panel):
    rows_dev = lax.axis_size("row")
    cols_dev = lax.axis_size("col")
    my_row = lax.axis_index("row")
    my_col = lax.axis_index("col")
    loc_rows, width, loc_cols, _unused_b = matrix.shape
    row_blocks = jnp.arange(loc_rows, dtype=jnp.int32) * rows_dev + my_row
    col_local = panel // cols_dev
    row_local = panel // rows_dev
    owner_row = panel % rows_dev
    owner_col = panel % cols_dev
    column_strip = lax.dynamic_index_in_dim(matrix, col_local, 2, keepdims=False)
    diag_raw = lax.dynamic_index_in_dim(column_strip, row_local, 0, keepdims=False)
    factor = picked(jnp.linalg.cholesky(diag_raw), "row", owner_row)
    flat_rows = column_strip.reshape(loc_rows * width, width)
    solved = jax.scipy.linalg.solve_triangular(factor, flat_rows.T, lower=True).T
    solved = solved.reshape(loc_rows, width, width)
    below_panel = (row_blocks > panel)[:, None, None]
    on_panel = (row_blocks == panel)[:, None, None]
    rows_local = jnp.where(below_panel, solved, jnp.float32(0.0))
    rows_part = from_root(rows_local, "col", owner_col)
    new_strip = jnp.where(below_panel, solved, column_strip)
    new_strip = jnp.where(on_panel, factor[None, :, :], new_strip)
    written = jnp.where(my_col == owner_col, new_strip, column_strip)
    matrix = lax.dynamic_update_index_in_dim(matrix, written, col_local, 2)
    stride_ratio = cols_dev // rows_dev
    source_row = my_col % rows_dev
    offset_pick = my_col // rows_dev
    received = broadcast_by_parts(rows_part, "row", source_row)
    grouped = received.reshape(loc_cols, stride_ratio, width, width)
    cols_part = lax.dynamic_index_in_dim(grouped, offset_pick, 1, keepdims=False)
    return (rows_part, cols_part, matrix)


def per_device(matrix_in, panel_start):
    first_panel = panel_start[0]
    matrix = matrix_in
    cols_dev = lax.axis_size("col")
    loc_rows, width, loc_cols, _unused_c = matrix.shape
    rows_first, cols_first, matrix = factor_panel(matrix, first_panel)
    next_panel = first_panel + 1
    col_next = next_panel // cols_dev
    next_strip = lax.dynamic_index_in_dim(matrix, col_next, 2, keepdims=False)
    next_piece = lax.dynamic_index_in_dim(cols_first, col_next, 0, keepdims=False)
    left_panel = rows_first.reshape(loc_rows * width, width)
    strip_product = lax.dot_general(
        left_panel,
        next_piece,
        (((1,), (1,)), ((), ())),
        precision=lax.Precision.HIGHEST,
        preferred_element_type=jnp.float32,
    )
    next_strip = next_strip - strip_product.reshape(loc_rows, width, width)
    matrix = lax.dynamic_update_index_in_dim(matrix, next_strip, col_next, 2)
    rows_second, cols_second, matrix = factor_panel(matrix, next_panel)
    skipped = (jnp.arange(loc_cols, dtype=jnp.int32) == col_next)[:, None, None]
    cols_rest = jnp.where(skipped, jnp.float32(0.0), cols_first)
    matrix = update(matrix, rows_first, cols_rest)
    matrix = update(matrix, rows_second, cols_second)
    return matrix


def solution(mesh):
    return jax.shard_map(
        per_device,
        mesh=mesh,
        in_specs=(P(None, "row", None, "col"), P()),
        out_specs=P(None, "row", None, "col"),
        check_vma=False,
    )
```

profile of v0, /device:TPU:1, one launch (start us, length us, event | category | flops | bytes accessed | tf_op | source)
XLA Modules:
  0.0 873.0 jit_solution(14277893120988400959)
XLA Ops:
  11.3 11.7 %cholesky.286 = f32[128,128]{1,0:T(8,128)S(1)} custom-call(f32[128,128]{1,0:T(8,128)S(1)} %cholesky.426), custom_call_target="Cholesky" | custom-call | tf_op jit(solution)/shard_map/jit(cholesky)/cholesky | solution.py:60
  33.7 11.7 %cholesky.305 = f32[128,128]{1,0:T(8,128)S(1)} custom-call(f32[128,128]{1,0:T(8,128)S(1)} %cholesky.430), custom_call_target="Cholesky" | custom-call | tf_op jit(solution)/shard_map/jit(cholesky)/cholesky | solution.py:60
  45.4 10.0 %custom-call.28 = f32[1,128,128]{1,2,0:T(8,128)S(1)} custom-call(f32[1,128,128]{2,1,0:T(8,128)S(1)} %get-tuple-element.63), custom_call_target="InvertDiagBlocksLowerTriangular" | custom-call | tf_op jit(solution)/shard_map/jit(cholesky)/cholesky | solution.py:60
  56.1 11.7 %cholesky.326 = f32[128,128]{1,0:T(8,128)S(1)} custom-call(f32[128,128]{1,0:T(8,128)S(1)} %cholesky.435), custom_call_target="Cholesky" | custom-call | tf_op jit(solution)/shard_map/jit(cholesky)/cholesky | solution.py:60
  78.9 11.7 %cholesky.343 = f32[128,128]{1,0:T(8,128)S(1)} custom-call(f32[128,128]{1,0:T(8,128)S(1)} %convolution_subtract_fusion.9), custom_call_target="Cholesky" | custom-call | tf_op jit(solution)/shard_map/jit(cholesky)/cholesky | solution.py:60
  109.0 40.4 %all-gather.11.cloned.1.call-done = f32[4096,512]{1,0:T(8,128)} async-done(((f32[512,512]{1,0:T(8,128)}), f32[4096,512]{1,0:T(8,128)}) %all-gather.11.cloned.1.call-update) | async-done | bytes 8388624 | tf_op jit(solution)/shard_map/all_gather | solution.py:8
  159.2 39.7 %custom-call.30 = f32[4,128,128]{1,2,0:T(8,128)S(1)} custom-call(f32[4,128,128]{2,1,0:T(8,128)S(1)} %get-tuple-element.21), custom_call_target="InvertDiagBlocksLowerTriangular" | custom-call | tf_op jit(solution)/shard_map/jit(_solve_triangular)/triangular_solve | solution.py:62
  229.5 103.3 %all-reduce.4.cloned.1.call-done = f32[4,512,512]{2,1,0:T(8,128)} async-done(((f32[4,512,512]{2,1,0:T(8,128)}), f32[4,512,512]{2,1,0:T(8,128)}) %all-reduce.4.cloned.1.call-update) | async-done | bytes 4194320 | tf_op jit(solution)/shard_map/psum | solution.py:13
  335.3 36.9 %reduce-scatter.3.cloned.1.call-done = f32[256,512]{1,0:T(8,128)} async-done(((f32[2048,512]{1,0:T(8,128)}), f32[256,512]{1,0:T(8,128)}) %reduce-scatter.3.cloned.1.call-update) | async-done | bytes 524304 | tf_op jit(solution)/shard_map/reduce_scatter | solution.py:28
  383.7 24.3 %all-gather.7.cloned.1.call-done = f32[2048,512]{1,0:T(8,128)} async-done(((f32[256,512]{1,0:T(8,128)}), f32[2048,512]{1,0:T(8,128)}) %all-gather.7.cloned.1.call-update) | async-done | bytes 4194320 | tf_op jit(solution)/shard_map/all_gather | solution.py:29
  408.0 11.0 %bitcast_dynamic-update-slice_fusion.2 = f32[4,512,2,512]{3,1,2,0:T(8,128)} fusion(f32[4,512,2,512]{3,1,2,0:T(8,128)} %select_dynamic-update-slice_fusion.1, s32[]{:T(128)S(6)} %select_n.178, f32[4,512,1,512]{3,1,2,0:T(8,128)} %constant_dynamic-slice_fusion.4, f32[4,512,512]{2,1,0:T(8,128)} %all-reduce.4.cloned.1.call-done, ...), kind=kOutput, calls=%fused_computation.11 | convolution fusion | flops 6443499520 | bytes 13631500 | tf_op jit(solution)/shard_map/dot_general | solution.py:92
  422.1 11.7 %cholesky.358 = f32[128,128]{1,0:T(8,128)S(1)} custom-call(f32[128,128]{1,0:T(8,128)S(1)} %cholesky.439), custom_call_target="Cholesky" | custom-call | tf_op jit(solution)/shard_map/jit(cholesky)/cholesky | solution.py:60
  445.1 11.7 %cholesky.377 = f32[128,128]{1,0:T(8,128)S(1)} custom-call(f32[128,128]{1,0:T(8,128)S(1)} %cholesky.443), custom_call_target="Cholesky" | custom-call | tf_op jit(solution)/shard_map/jit(cholesky)/cholesky | solution.py:60
  457.6 10.2 %custom-call.32 = f32[1,128,128]{1,2,0:T(8,128)S(1)} custom-call(f32[1,128,128]{2,1,0:T(8,128)S(1)} %get-tuple-element.53), custom_call_target="InvertDiagBlocksLowerTriangular" | custom-call | tf_op jit(solution)/shard_map/jit(cholesky)/cholesky | solution.py:60
  468.5 11.7 %cholesky.398 = f32[128,128]{1,0:T(8,128)S(1)} custom-call(f32[128,128]{1,0:T(8,128)S(1)} %cholesky.448), custom_call_target="Cholesky" | custom-call | tf_op jit(solution)/shard_map/jit(cholesky)/cholesky | solution.py:60
  491.3 11.7 %cholesky.415 = f32[128,128]{1,0:T(8,128)S(1)} custom-call(f32[128,128]{1,0:T(8,128)S(1)} %convolution_subtract_fusion.8), custom_call_target="Cholesky" | custom-call | tf_op jit(solution)/shard_map/jit(cholesky)/cholesky | solution.py:60
  512.2 45.1 %all-gather.13.cloned.1.call-done = f32[4096,512]{1,0:T(8,128)} async-done(((f32[512,512]{1,0:T(8,128)}), f32[4096,512]{1,0:T(8,128)}) %all-gather.13.cloned.1.call-update) | async-done | bytes 8388624 | tf_op jit(solution)/shard_map/all_gather | solution.py:8
  566.7 39.3 %custom-call.34 = f32[4,128,128]{1,2,0:T(8,128)S(1)} custom-call(f32[4,128,128]{2,1,0:T(8,128)S(1)} %get-tuple-element.22), custom_call_target="InvertDiagBlocksLowerTriangular" | custom-call | tf_op jit(solution)/shard_map/jit(_solve_triangular)/triangular_solve | solution.py:62
  636.8 103.3 %all-reduce.6.cloned.1.call-done = f32[4,512,512]{2,1,0:T(8,128)} async-done(((f32[4,512,512]{2,1,0:T(8,128)}), f32[4,512,512]{2,1,0:T(8,128)}) %all-reduce.6.cloned.1.call-update) | async-done | bytes 4194320 | tf_op jit(solution)/shard_map/psum | solution.py:13
  742.6 36.9 %reduce-scatter.5.cloned.1.call-done = f32[256,512]{1,0:T(8,128)} async-done(((f32[2048,512]{1,0:T(8,128)}), f32[256,512]{1,0:T(8,128)}) %reduce-scatter.5.cloned.1.call-update) | async-done | bytes 524304 | tf_op jit(solution)/shard_map/reduce_scatter | solution.py:28
  786.3 29.1 %all-gather.9.cloned.1.call-done = f32[2048,512]{1,0:T(8,128)} async-done(((f32[256,512]{1,0:T(8,128)}), f32[2048,512]{1,0:T(8,128)}) %all-gather.9.cloned.1.call-update) | async-done | bytes 4194320 | tf_op jit(solution)/shard_map/all_gather | solution.py:29
  815.5 17.0 %fusion = f32[4,512,2,512]{3,1,2,0:T(8,128)S(1)} fusion(f32[4,512,512]{2,1,0:T(8,128)} %all-reduce.6.cloned.1.call-done, f32[2,2,512,512]{3,2,1,0:T(8,128)} %bitcast.194, s32[]{:T(128)S(6)} %select_n.187), kind=kOutput, calls=%fused_computation.7 | convolution fusion | flops 12884901888 | bytes 14680068 | tf_op jit(solution)/shard_map/dot_general | solution.py:37
  832.5 18.1 %subtract_subtract_fusion = f32[4,512,2,512]{3,1,2,0:T(8,128)} fusion(f32[4,512,2,512]{3,1,2,0:T(8,128)S(1)} %fusion, f32[4,512,2,512]{3,1,2,0:T(8,128)S(1)} %copy-done, f32[4,512,512]{2,1,0:T(8,128)S(1)} %copy-done.1, f32[2,2,512,512]{3,2,1,0:T(8,128)} %bitcast.193, s32[]{:T(128)S(6)} %select_n.187, pred[2]{0:T(512)(128)(4,1)S(1)} %iota_compare_fusion.3), kind=kOutput, calls=%fused_computation.4 | convolution fusion | flops 12889620480 | bytes 31457286 | tf_op jit(solution)/shard_map/dot_general | solution.py:37
  850.6 15.4 %copy.15 = f32[4,512,2,512]{3,2,1,0:T(2,128)} copy(f32[4,512,2,512]{3,1,2,0:T(8,128)} %subtract_subtract_fusion) | data formatting | bytes 16777216 | tf_op jit(solution)/shard_map/sub | solution.py:44
  (135 shorter events, 195.1 us)
Async XLA Ops:
  6.5 142.9 %all-gather.11.cloned.1.call-start = ((), (), s32[]{:S(2)}) async-start(), calls=%async_computation.8 | async-start | bytes 9437184 | tf_op jit(solution)/shard_map/all_gather | solution.py:8
  96.0 236.8 %all-reduce.4.cloned.1.call-start = ((), (), s32[]{:S(2)}) async-start(), calls=%async_computation.2 | async-start | bytes 8388608 | tf_op jit(solution)/shard_map/psum | solution.py:13
  198.9 6.6 copy-start.3
  229.4 142.7 %reduce-scatter.3.cloned.1.call-start = ((), (), s32[]{:S(2)}) async-start(), calls=%async_computation.3 | async-start | bytes 4718592 | tf_op jit(solution)/shard_map/reduce_scatter | solution.py:28
  335.3 72.8 %all-gather.7.cloned.1.call-start = ((), (), s32[]{:S(2)}) async-start(), calls=%async_computation.4 | async-start | bytes 4718592 | tf_op jit(solution)/shard_map/all_gather | solution.py:29
  372.2 185.1 %all-gather.13.cloned.1.call-start = ((), (), s32[]{:S(2)}) async-start(), calls=%async_computation.9 | async-start | bytes 9437184 | tf_op jit(solution)/shard_map/all_gather | solution.py:8
  507.6 232.5 %all-reduce.6.cloned.1.call-start = ((), (), s32[]{:S(2)}) async-start(), calls=%async_computation.5 | async-start | bytes 8388608 | tf_op jit(solution)/shard_map/psum | solution.py:13
  606.0 6.6 copy-start.2
  636.8 142.7 %reduce-scatter.5.cloned.1.call-start = ((), (), s32[]{:S(2)}) async-start(), calls=%async_computation.6 | async-start | bytes 4718592 | tf_op jit(solution)/shard_map/reduce_scatter | solution.py:28
  742.5 72.9 %all-gather.9.cloned.1.call-start = ((), (), s32[]{:S(2)}) async-start(), calls=%async_computation.7 | async-start | bytes 4718592 | tf_op jit(solution)/shard_map/all_gather | solution.py:29
  815.5 17.0 %copy-start = (f32[4,512,2,512]{3,1,2,0:T(8,128)S(1)}, f32[4,512,2,512]{3,1,2,0:T(8,128)}, u32[]{:S(2)}) copy-start(f32[4,512,2,512]{3,1,2,0:T(8,128)} %select_dynamic-update-slice_fusion) | copy-start | bytes 25165828
  815.5 17.0 %copy-start.1 = (f32[4,512,512]{2,1,0:T(8,128)S(1)}, f32[4,512,512]{2,1,0:T(8,128)}, u32[]{:S(2)}) copy-start(f32[4,512,512]{2,1,0:T(8,128)} %all-reduce.4.cloned.1.call-done) | copy-start | bytes 12582916
Sparse Core Ops, SparseCore 0:
  96.1 53.2 all-gather.10
  229.5 103.1 all-reduce.3
  335.4 36.7 reduce-scatter.2
  373.7 34.2 all-gather.6
  507.7 49.6 all-gather.12
  636.9 103.1 all-reduce.5
  742.7 36.7 reduce-scatter.4
  781.2 34.2 all-gather.8
where the time goes:
time: 883 us; the launch traced here: 873 us
  waiting for transfers between devices  419 us (47%)
  other arithmetic  278 us (31%)
  matrix products  85.5 us (10%)
  local copies, waits for them, and re-layouts  69.8 us (8%)
  between operations  20.2 us (2%)
    psum x2, waiting for transfers between devices, from_root(): return lax.psum(kept, axis)  207 us
    another operation x29, other arithmetic, factor_panel(): factor = picked(jnp.linalg.cholesky(diag_raw), 'row', owner_row)  158 us
    all_gather x2, waiting for transfers between devices, picked(): lax.all_gather(x, axis)  85.5 us
    another operation x5, other arithmetic, factor_panel(): jax.scipy.linalg.solve_triangular(factor, flat_rows.T, lower=True)  82 us
    reduce_scatter x2, waiting for transfers between devices, broadcast_by_parts(): own = lax.psum_scatter(padded, axis, scatter_dimension=0, tiled=True)  73.7 us
    all_gather x2, waiting for transfers between devices, broadcast_by_parts(): lax.all_gather(own, axis, axis=0, tiled=True)[:len(lines)].reshape(x.shape)  53.5 us
    another operation x14, matrix products, factor_panel(): jax.scipy.linalg.solve_triangular(factor, flat_rows.T, lower=True)  35.7 us
    dot_general x2, matrix products, update(): lax.dot_general(left_panel, right_panel, (((1,), (1,)), ((), ())), precis...  35.1 us
  transfers between devices with their start and end apart: 8, of which 8 were waited for; matrix products, arithmetic and copies ran while one was open for 4% of the time, Pallas kernels for 0%

commit v1 on v0

--- a/solution.py
+++ b/solution.py
@@ -26,7 +26,9 @@
     )
     padded = padded_to(lines, lax.axis_size(axis))
     own = lax.psum_scatter(padded, axis, scatter_dimension=0, tiled=True)
-    return lax.all_gather(own, axis, axis=0, tiled=True)[: len(lines)].reshape(x.shape)
+    return jnp.concatenate(
+        lax.all_to_all(jnp.stack([own] * lax.axis_size(axis)), axis, 0, 0), axis=0
+    )[: len(lines)].reshape(x.shape)
 
 
 def update(matrix, rows_part, cols_part):

time: 883 us -> 932 us (1.055)
  waiting for transfers between devices: 419 us -> 445 us
  starting transfers between devices: 0.29 us -> 16.2 us
    all_to_all x0 -> x2, waiting for transfers between devices: none -> 79.3 us  [broadcast_by_parts(): lax.all_to_all(jnp.stack([own] * lax.axis_size(axis)), axis, 0, 0)]
    all_gather x2 -> x0, waiting for transfers between devices: 53.5 us -> none  [broadcast_by_parts(): lax.all_gather(own, axis, axis=0, tiled=True)[:len(lines)].reshape(x.shape)]
    all_to_all x0 -> x2, starting transfers between devices: none -> 16 us  [broadcast_by_parts(): lax.all_to_all(jnp.stack([own] * lax.axis_size(axis)), axis, 0, 0)]
where the time goes in v1:
time: 932 us; the launch traced here: 922 us
  waiting for transfers between devices  445 us (48%)
  other arithmetic  277 us (30%)
  matrix products  85.5 us (9%)
  local copies, waits for them, and re-layouts  77.3 us (8%)
  between operations  20 us (2%)
  starting transfers between devices  16.2 us (2%)
    psum x2, waiting for transfers between devices, from_root(): return lax.psum(kept, axis)  207 us
    another operation x29, other arithmetic, factor_panel(): factor = picked(jnp.linalg.cholesky(diag_raw), 'row', owner_row)  158 us
    all_gather x2, waiting for transfers between devices, picked(): lax.all_gather(x, axis)  85.7 us
    another operation x5, other arithmetic, factor_panel(): jax.scipy.linalg.solve_triangular(factor, flat_rows.T, lower=True)  81.8 us
    all_to_all x2, waiting for transfers between devices, broadcast_by_parts(): lax.all_to_all(jnp.stack([own] * lax.axis_size(axis)), axis, 0, 0)  79.3 us
    reduce_scatter x2, waiting for transfers between devices, broadcast_by_parts(): own = lax.psum_scatter(padded, axis, scatter_dimension=0, tiled=True)  73.8 us
    another operation x14, matrix products, factor_panel(): jax.scipy.linalg.solve_triangular(factor, flat_rows.T, lower=True)  35.5 us
    dot_general x2, matrix products, update(): lax.dot_general(left_panel, right_panel, (((1,), (1,)), ((), ())), precis...  35.1 us
  transfers between devices with their start and end apart: 8, of which 8 were waited for; matrix products, arithmetic and copies ran while one was open for 4% of the time, Pallas kernels for 0%

profile of v1, /device:TPU:1, one launch (start us, length us, event | category | flops | bytes accessed | tf_op | source)
XLA Modules:
  0.0 921.7 jit_solution(13470864316961851794)
XLA Ops:
  11.3 11.7 %cholesky.286 = f32[128,128]{1,0:T(8,128)S(1)} custom-call(f32[128,128]{1,0:T(8,128)S(1)} %cholesky.426), custom_call_target="Cholesky" | custom-call | tf_op jit(solution)/shard_map/jit(cholesky)/cholesky | solution.py:62
  33.7 11.7 %cholesky.305 = f32[128,128]{1,0:T(8,128)S(1)} custom-call(f32[128,128]{1,0:T(8,128)S(1)} %cholesky.430), custom_call_target="Cholesky" | custom-call | tf_op jit(solution)/shard_map/jit(cholesky)/cholesky | solution.py:62
  45.4 10.1 %custom-call.28 = f32[1,128,128]{1,2,0:T(8,128)S(1)} custom-call(f32[1,128,128]{2,1,0:T(8,128)S(1)} %get-tuple-element.63), custom_call_target="InvertDiagBlocksLowerTriangular" | custom-call | tf_op jit(solution)/shard_map/jit(cholesky)/cholesky | solution.py:62
  56.2 11.7 %cholesky.326 = f32[128,128]{1,0:T(8,128)S(1)} custom-call(f32[128,128]{1,0:T(8,128)S(1)} %cholesky.435), custom_call_target="Cholesky" | custom-call | tf_op jit(solution)/shard_map/jit(cholesky)/cholesky | solution.py:62
  79.0 11.7 %cholesky.343 = f32[128,128]{1,0:T(8,128)S(1)} custom-call(f32[128,128]{1,0:T(8,128)S(1)} %convolution_subtract_fusion.9), custom_call_target="Cholesky" | custom-call | tf_op jit(solution)/shard_map/jit(cholesky)/cholesky | solution.py:62
  108.7 40.5 %all-gather.5.cloned.1.call-done = f32[4096,512]{1,0:T(8,128)} async-done(((f32[512,512]{1,0:T(8,128)}), f32[4096,512]{1,0:T(8,128)}) %all-gather.5.cloned.1.call-update) | async-done | bytes 8388624 | tf_op jit(solution)/shard_map/all_gather | solution.py:8
  158.9 39.5 %custom-call.30 = f32[4,128,128]{1,2,0:T(8,128)S(1)} custom-call(f32[4,128,128]{2,1,0:T(8,128)S(1)} %get-tuple-element.21), custom_call_target="InvertDiagBlocksLowerTriangular" | custom-call | tf_op jit(solution)/shard_map/jit(_solve_triangular)/triangular_solve | solution.py:64
  229.0 103.3 %all-reduce.4.cloned.1.call-done = f32[4,512,512]{2,1,0:T(8,128)} async-done(((f32[4,512,512]{2,1,0:T(8,128)}), f32[4,512,512]{2,1,0:T(8,128)}) %all-reduce.4.cloned.1.call-update) | async-done | bytes 4194320 | tf_op jit(solution)/shard_map/psum | solution.py:13
  334.7 36.9 %reduce-scatter.3.cloned.1.call-done = f32[256,512]{1,0:T(8,128)} async-done(((f32[2048,512]{1,0:T(8,128)}), f32[256,512]{1,0:T(8,128)}) %reduce-scatter.3.cloned.1.call-update) | async-done | bytes 524304 | tf_op jit(solution)/shard_map/reduce_scatter | solution.py:28
  394.6 37.3 %all-to-all-done = f32[8,256,512]{2,1,0:T(8,128)} async-done(((f32[8,256,512]{2,1,0:T(8,128)}), f32[8,256,512]{2,1,0:T(8,128)}, u32[]{:S(2)}, u32[]{:S(2)}) %all-to-all-start) | async-done | bytes 4194336 | tf_op jit(solution)/shard_map/all_to_all | solution.py:30
  432.0 11.1 %bitcast_dynamic-update-slice_fusion.2 = f32[4,512,2,512]{3,1,2,0:T(8,128)} fusion(f32[4,512,2,512]{3,1,2,0:T(8,128)} %select_dynamic-update-slice_fusion.1, s32[]{:T(128)S(6)} %select_n.178, f32[4,512,1,512]{3,1,2,0:T(8,128)} %constant_dynamic-slice_fusion.4, f32[4,512,512]{2,1,0:T(8,128)} %all-reduce.4.cloned.1.call-done, ...), kind=kOutput, calls=%fused_computation.11 | convolution fusion | flops 6443499520 | bytes 13631500 | tf_op jit(solution)/shard_map/dot_general | solution.py:94
  446.2 11.7 %cholesky.358 = f32[128,128]{1,0:T(8,128)S(1)} custom-call(f32[128,128]{1,0:T(8,128)S(1)} %cholesky.439), custom_call_target="Cholesky" | custom-call | tf_op jit(solution)/shard_map/jit(cholesky)/cholesky | solution.py:62
  469.2 11.7 %cholesky.377 = f32[128,128]{1,0:T(8,128)S(1)} custom-call(f32[128,128]{1,0:T(8,128)S(1)} %cholesky.443), custom_call_target="Cholesky" | custom-call | tf_op jit(solution)/shard_map/jit(cholesky)/cholesky | solution.py:62
  481.6 9.9 %custom-call.32 = f32[1,128,128]{1,2,0:T(8,128)S(1)} custom-call(f32[1,128,128]{2,1,0:T(8,128)S(1)} %get-tuple-element.53), custom_call_target="InvertDiagBlocksLowerTriangular" | custom-call | tf_op jit(solution)/shard_map/jit(cholesky)/cholesky | solution.py:62
  492.3 11.7 %cholesky.398 = f32[128,128]{1,0:T(8,128)S(1)} custom-call(f32[128,128]{1,0:T(8,128)S(1)} %cholesky.448), custom_call_target="Cholesky" | custom-call | tf_op jit(solution)/shard_map/jit(cholesky)/cholesky | solution.py:62
  515.1 11.7 %cholesky.415 = f32[128,128]{1,0:T(8,128)S(1)} custom-call(f32[128,128]{1,0:T(8,128)S(1)} %convolution_subtract_fusion.8), custom_call_target="Cholesky" | custom-call | tf_op jit(solution)/shard_map/jit(cholesky)/cholesky | solution.py:62
  536.0 45.3 %all-gather.7.cloned.1.call-done = f32[4096,512]{1,0:T(8,128)} async-done(((f32[512,512]{1,0:T(8,128)}), f32[4096,512]{1,0:T(8,128)}) %all-gather.7.cloned.1.call-update) | async-done | bytes 8388624 | tf_op jit(solution)/shard_map/all_gather | solution.py:8
  591.1 39.3 %custom-call.34 = f32[4,128,128]{1,2,0:T(8,128)S(1)} custom-call(f32[4,128,128]{2,1,0:T(8,128)S(1)} %get-tuple-element.22), custom_call_target="InvertDiagBlocksLowerTriangular" | custom-call | tf_op jit(solution)/shard_map/jit(_solve_triangular)/triangular_solve | solution.py:64
  661.0 103.3 %all-reduce.6.cloned.1.call-done = f32[4,512,512]{2,1,0:T(8,128)} async-done(((f32[4,512,512]{2,1,0:T(8,128)}), f32[4,512,512]{2,1,0:T(8,128)}) %all-reduce.6.cloned.1.call-update) | async-done | bytes 4194320 | tf_op jit(solution)/shard_map/psum | solution.py:13
  766.7 36.9 %reduce-scatter.5.cloned.1.call-done = f32[256,512]{1,0:T(8,128)} async-done(((f32[2048,512]{1,0:T(8,128)}), f32[256,512]{1,0:T(8,128)}) %reduce-scatter.5.cloned.1.call-update) | async-done | bytes 524304 | tf_op jit(solution)/shard_map/reduce_scatter | solution.py:28
  822.1 41.9 %all-to-all-done.1 = f32[8,256,512]{2,1,0:T(8,128)} async-done(((f32[8,256,512]{2,1,0:T(8,128)}), f32[8,256,512]{2,1,0:T(8,128)}, u32[]{:S(2)}, u32[]{:S(2)}) %all-to-all-start.1) | async-done | bytes 4194336 | tf_op jit(solution)/shard_map/all_to_all | solution.py:30
  864.0 17.0 %fusion = f32[4,512,2,512]{3,1,2,0:T(8,128)S(1)} fusion(f32[4,512,512]{2,1,0:T(8,128)} %all-reduce.6.cloned.1.call-done, f32[2,2,512,512]{3,2,1,0:T(8,128)} %bitcast.57, s32[]{:T(128)S(6)} %select_n.187), kind=kOutput, calls=%fused_computation.7 | convolution fusion | flops 12884901888 | bytes 14680068 | tf_op jit(solution)/shard_map/dot_general | solution.py:39
  881.0 18.1 %subtract_subtract_fusion = f32[4,512,2,512]{3,1,2,0:T(8,128)} fusion(f32[4,512,2,512]{3,1,2,0:T(8,128)S(1)} %fusion, f32[4,512,2,512]{3,1,2,0:T(8,128)S(1)} %copy-done, f32[4,512,512]{2,1,0:T(8,128)S(1)} %copy-done.1, f32[2,2,512,512]{3,2,1,0:T(8,128)} %bitcast.24, s32[]{:T(128)S(6)} %select_n.187, pred[2]{0:T(512)(128)(4,1)S(1)} %iota_compare_fusion.3), kind=kOutput, calls=%fused_computation.4 | convolution fusion | flops 12889620480 | bytes 31457286 | tf_op jit(solution)/shard_map/dot_general | solution.py:39
  899.1 15.4 %copy.26 = f32[4,512,2,512]{3,2,1,0:T(2,128)} copy(f32[4,512,2,512]{3,1,2,0:T(8,128)} %subtract_subtract_fusion) | data formatting | bytes 16777216 | tf_op jit(solution)/shard_map/sub | solution.py:46
  (135 shorter events, 218.5 us)
Async XLA Ops:
  6.5 142.6 %all-gather.5.cloned.1.call-start = ((), (), s32[]{:S(2)}) async-start(), calls=%async_computation.8 | async-start | bytes 9437184 | tf_op jit(solution)/shard_map/all_gather | solution.py:8
  95.7 236.5 %all-reduce.4.cloned.1.call-start = ((), (), s32[]{:S(2)}) async-start(), calls=%async_computation.4 | async-start | bytes 8388608 | tf_op jit(solution)/shard_map/psum | solution.py:13
  198.4 6.6 copy-start.3
  228.9 142.7 %reduce-scatter.3.cloned.1.call-start = ((), (), s32[]{:S(2)}) async-start(), calls=%async_computation.5 | async-start | bytes 4718592 | tf_op jit(solution)/shard_map/reduce_scatter | solution.py:28
  375.1 56.8 %all-to-all-start = ((f32[8,256,512]{2,1,0:T(8,128)}), f32[8,256,512]{2,1,0:T(8,128)}, u32[]{:S(2)}, u32[]{:S(2)}) async-start(f32[8,256,512]{2,1,0:T(8,128)} %stack.4), calls=%async_computation.1 | async-start | bytes 8388608 | tf_op jit(solution)/shard_map/all_to_all | solution.py:30
  383.1 198.2 %all-gather.7.cloned.1.call-start = ((), (), s32[]{:S(2)}) async-start(), calls=%async_computation.9 | async-start | bytes 9437184 | tf_op jit(solution)/shard_map/all_gather | solution.py:8
  531.3 232.9 %all-reduce.6.cloned.1.call-start = ((), (), s32[]{:S(2)}) async-start(), calls=%async_computation.6 | async-start | bytes 8388608 | tf_op jit(solution)/shard_map/psum | solution.py:13
  630.4 6.6 copy-start.2
  660.9 142.7 %reduce-scatter.5.cloned.1.call-start = ((), (), s32[]{:S(2)}) async-start(), calls=%async_computation.7 | async-start | bytes 4718592 | tf_op jit(solution)/shard_map/reduce_scatter | solution.py:28
  807.2 56.8 %all-to-all-start.1 = ((f32[8,256,512]{2,1,0:T(8,128)}), f32[8,256,512]{2,1,0:T(8,128)}, u32[]{:S(2)}, u32[]{:S(2)}) async-start(f32[8,256,512]{2,1,0:T(8,128)} %stack.5), calls=%async_computation.3 | async-start | bytes 8388608 | tf_op jit(solution)/shard_map/all_to_all | solution.py:30
  864.0 17.0 %copy-start = (f32[4,512,2,512]{3,1,2,0:T(8,128)S(1)}, f32[4,512,2,512]{3,1,2,0:T(8,128)}, u32[]{:S(2)}) copy-start(f32[4,512,2,512]{3,1,2,0:T(8,128)} %select_dynamic-update-slice_fusion) | copy-start | bytes 25165828
  864.0 17.0 %copy-start.1 = (f32[4,512,512]{2,1,0:T(8,128)S(1)}, f32[4,512,512]{2,1,0:T(8,128)}, u32[]{:S(2)}) copy-start(f32[4,512,512]{2,1,0:T(8,128)} %all-reduce.4.cloned.1.call-done) | copy-start | bytes 12582916
Sparse Core Ops, SparseCore 0:
  95.9 53.2 all-gather.4
  229.0 103.1 all-reduce.3
  334.8 36.7 reduce-scatter.2
  531.4 49.8 all-gather.6
  661.1 103.1 all-reduce.5
  766.9 36.7 reduce-scatter.4
